TPU v7x, 32 devices: a whole 2x2x4 slice. The times are simulated.
32 devices in a mesh: dp: 8 (over z, x), tensor: 4 (over y, core).
Axes of the slice: x: 2, y: 2, z: 4, core: 2. Of those that a mesh axis runs over, the one named last changes fastest.
Arguments:
- hidden_in: bfloat16 [4096, 2048], P('dp'), may hold values from -40 to 40
- seq_lens: int32 [8, 8], P('dp'), may hold values from 0 to 512, as said below
- norm1_gain: float32 [2048], replicated, may hold values from 0.5 to 1.5
- query_weight: bfloat16 [2048, 4096], P(None, 'tensor'), may hold values from -0.125 to 0.125
- key_weight: bfloat16 [2048, 512], P(None, 'tensor'), may hold values from -0.125 to 0.125
- value_weight: bfloat16 [2048, 512], P(None, 'tensor'), may hold values from -0.125 to 0.125
- query_gain: float32 [128], replicated, may hold values from 0.5 to 1.5
- key_gain: float32 [128], replicated, may hold values from 0.5 to 1.5
- out_weight: bfloat16 [4096, 2048], P('tensor'), may hold values from -0.75 to 0.75
- norm2_gain: float32 [2048], replicated, may hold values from 0.5 to 1.5
- w_gate_up: bfloat16 [16, 2048, 2, 768], P('dp', None, None, 'tensor'), may hold values from -0.125 to 0.125
- w_down: bfloat16 [16, 768, 2048], P('dp', 'tensor'), may hold values from -0.875 to 0.875
- routes: int32 [4096, 8], P('dp'), may hold values from 0 to 15, all different within a row; in each aligned block of 512 rows (0 to 511, 512 to 1023, ...) at most 384 rows name the same one
- route_weights: float32 [4096, 8], P('dp'), may hold values from 0.05 to 0.25
- out_grad: bfloat16 [4096, 2048], P('dp'), may hold values from -6 to 6
Outputs:
- hidden_out: bfloat16 [4096, 2048], P('dp')
- hidden_grad: bfloat16 [4096, 2048], P('dp')
- grad_norm1_gain: float32 [2048], replicated
- grad_query_weight: float32 [2048, 4096], P(None, 'tensor')
- grad_key_weight: float32 [2048, 512], P(None, 'tensor')
- grad_value_weight: float32 [2048, 512], P(None, 'tensor')
- grad_query_gain: float32 [128], replicated
- grad_key_gain: float32 [128], replicated
- grad_out_weight: float32 [4096, 2048], P('tensor')
- grad_norm2_gain: float32 [2048], replicated
- grad_w_gate_up: float32 [16, 2048, 2, 768], P('dp', None, None, 'tensor')
- grad_w_down: float32 [16, 768, 2048], P('dp', 'tensor')
Inputs may be any that keep to these rules, and one draw needn't show every extreme that they name: `seq_lens`: each row sums to 512; zeros are empty slots; some row holds a single sequence of 512. `routes`: A row names 8 different experts. In the rows of one index of dp no expert is named by more than 384 rows, a bound that some block reaches.
All inputs are finite; a program needn't handle non-finite values.
Results may differ from a plain program's by a relative error of at most 0.028.
Values may be sent and summed in bfloat16 or wider, within the bound.
A program may use at most 384 MiB of HBM per device.

v0:
```python
import math
import jax
import jax.numpy as jnp
from jax import lax
from jax.sharding import PartitionSpec as P

EPSILON = 1e-06
ROPE_BASE = 1000000.0


def rms_parts(values):
    inverse = lax.rsqrt(jnp.mean(values * values, axis=-1, keepdims=True) + EPSILON)
    return (values * inverse, inverse)


def rms_back(grad_hat, normal_hat, inverse):
    return inverse * (
        grad_hat - normal_hat * jnp.mean(grad_hat * normal_hat, axis=-1, keepdims=True)
    )


def rotary_tables(positions, head_dim):
    halves = jnp.arange(head_dim // 2, dtype=jnp.float32)
    inverse = jnp.exp(halves * (-2.0 * math.log(ROPE_BASE) / head_dim))
    angles = positions.astype(jnp.float32)[:, None] * inverse[None, :]
    return (jnp.cos(angles), jnp.sin(angles))


def rotate(values, cosine_table, sine_table):
    middle_index = values.shape[-1] // 2
    first_half = values[..., :middle_index]
    second = values[..., middle_index:]
    return jnp.concatenate(
        [
            first_half * cosine_table - second * sine_table,
            second * cosine_table + first_half * sine_table,
        ],
        axis=-1,
    )


def rotate_back(gradient, cosine_table, sine_table):
    middle_index = gradient.shape[-1] // 2
    first_half = gradient[..., :middle_index]
    second = gradient[..., middle_index:]
    return jnp.concatenate(
        [
            first_half * cosine_table + second * sine_table,
            second * cosine_table - first_half * sine_table,
        ],
        axis=-1,
    )


def sequence_layout(lengths, token_count):
    endings = jnp.cumsum(lengths)
    places = jnp.arange(token_count, dtype=jnp.int32)
    starts = jnp.sum(jnp.where(endings[None, :] <= places[:, None], lengths[None, :], 0), axis=1)
    return (places, starts)


def local(
    hidden_in,
    seq_lens,
    norm1_gain,
    query_weight,
    key_weight,
    value_weight,
    query_gain,
    key_gain,
    out_weight,
    norm2_gain,
    w_gate_up,
    w_down,
    routes,
    route_weights,
    out_grad,
):
    bf = jnp.bfloat16
    f32 = jnp.float32
    tokens, model_width = hidden_in.shape
    local_experts = w_gate_up.shape[0]
    hidden_part = w_gate_up.shape[3]
    head_dim = query_gain.shape[0]
    local_heads = query_weight.shape[1] // head_dim
    data_size = lax.axis_size("dp")
    tensor_size = lax.axis_size("tensor")
    quarter = tokens // tensor_size
    experts = local_experts * data_size
    score_scale = head_dim ** (-0.5)
    row0 = lax.axis_index("tensor") * quarter

    def mine(array):
        return lax.dynamic_slice_in_dim(array, row0, quarter, 0)

    expert_ids = jnp.arange(experts, dtype=jnp.int32)
    dense = jnp.sum(
        jnp.where(
            mine(routes)[:, :, None] == expert_ids[None, None, :],
            mine(route_weights)[:, :, None],
            0.0,
        ),
        axis=1,
    )
    dense_high = dense.astype(bf)
    dense_low = (dense - dense_high.astype(f32)).astype(bf)
    packed = jnp.concatenate([mine(out_grad), dense_high, dense_low], axis=1)
    gathered = lax.all_gather(packed, "dp", tiled=True)
    grads_all = gathered[:, :model_width]
    dense_all = gathered[:, model_width : model_width + experts].astype(f32) + gathered[
        :, model_width + experts :
    ].astype(f32)
    weight_all = lax.dynamic_slice_in_dim(
        dense_all, lax.axis_index("dp") * local_experts, local_experts, 1
    )
    rows = data_size * quarter
    units = local_experts * hidden_part
    own_weights = jnp.concatenate(
        [
            jnp.transpose(w_gate_up, (2, 0, 3, 1)).reshape(2, units, model_width),
            w_down.reshape(1, units, model_width),
        ],
        axis=0,
    )
    all_weights = lax.all_gather(own_weights, "tensor")
    weight_cols = jnp.broadcast_to(
        weight_all[:, None, :, None], (rows, tensor_size, local_experts, hidden_part)
    ).reshape(rows, tensor_size, units)
    hidden = hidden_in.astype(f32)
    hat_one, inv_one = rms_parts(hidden)
    normed = (hat_one * norm1_gain).astype(bf)
    query_proj = jnp.dot(normed, query_weight, preferred_element_type=f32).reshape(
        tokens, local_heads, head_dim
    )
    key_proj = jnp.dot(normed, key_weight, preferred_element_type=f32)
    value_low = jnp.dot(normed, value_weight, preferred_element_type=f32).astype(bf)
    places, starts = sequence_layout(seq_lens[0], tokens)
    cosine_table, sine_table = rotary_tables(places - starts, head_dim)
    query_hat, query_inv = rms_parts(query_proj)
    query_low = rotate(
        query_hat * query_gain, cosine_table[:, None, :], sine_table[:, None, :]
    ).astype(bf)
    key_hat, key_inv = rms_parts(key_proj)
    key_low = rotate(key_hat * key_gain, cosine_table, sine_table).astype(bf)
    visible = (places[None, :] <= places[:, None]) & (places[None, :] >= starts[:, None])
    scores = jnp.einsum("thd,sd->hts", query_low, key_low, preferred_element_type=f32) * score_scale
    exponent = jnp.where(visible[None], jnp.exp(scores), 0.0)
    totals = jnp.sum(exponent, axis=-1, keepdims=True)
    log_totals = jnp.log(totals)
    soft_low = (exponent / totals).astype(bf)
    mixed_low = (
        jnp.einsum("hts,sd->thd", soft_low, value_low, preferred_element_type=f32)
        .reshape(tokens, local_heads * head_dim)
        .astype(bf)
    )
    attention = lax.psum_scatter(
        jnp.dot(mixed_low, out_weight, preferred_element_type=f32).astype(bf), "tensor", tiled=True
    ).astype(f32)
    hidden_q = mine(hidden_in).astype(f32)
    hat_one_q, inv_one_q = rms_parts(hidden_q)
    middle = hidden_q + attention
    hat_two, inv_two = rms_parts(middle)
    normed_two = (hat_two * norm2_gain).astype(bf)
    inputs = lax.all_gather(normed_two, "dp", tiled=True)

    def project(left, which):
        return jnp.einsum("td,rud->tru", left, all_weights[:, which], preferred_element_type=f32)

    gate_act = project(inputs, 0)
    upward = project(inputs, 1)
    sigmoid_gate = jax.nn.sigmoid(gate_act)
    active = gate_act * sigmoid_gate * upward
    weighted_low = (weight_cols * active).astype(bf)
    mixture_part = jnp.einsum(
        "tru,rud->td", weighted_low, all_weights[:, 2], preferred_element_type=f32
    ).astype(bf)
    mixture = lax.psum_scatter(mixture_part, "dp", tiled=True).astype(f32)
    hidden_out = (middle + mixture).astype(bf)
    grad_active = weight_cols * project(grads_all, 2)
    grad_gate = (
        grad_active * upward * sigmoid_gate * (1.0 + gate_act * (1.0 - sigmoid_gate))
    ).astype(bf)
    grad_up = (grad_active * gate_act * sigmoid_gate).astype(bf)
    grad_normed_part = jnp.einsum(
        "tru,rud->td", grad_gate, all_weights[:, 0], preferred_element_type=f32
    ) + jnp.einsum("tru,rud->td", grad_up, all_weights[:, 1], preferred_element_type=f32)
    grad_normed_two = lax.psum_scatter(grad_normed_part.astype(bf), "dp", tiled=True).astype(f32)
    weight_grads = jnp.stack(
        [
            jnp.einsum("tru,td->rud", grad_gate, inputs, preferred_element_type=f32).astype(bf),
            jnp.einsum("tru,td->rud", grad_up, inputs, preferred_element_type=f32).astype(bf),
            jnp.einsum("tru,td->rud", weighted_low, grads_all, preferred_element_type=f32).astype(
                bf
            ),
        ],
        axis=1,
    )
    own_grads = (
        lax.psum_scatter(weight_grads.reshape(-1, model_width), "tensor", tiled=True)
        .astype(f32)
        .reshape(3, units, model_width)
    )
    grad_w_gate_up = jnp.transpose(
        own_grads[:2].reshape(2, local_experts, hidden_part, model_width), (1, 3, 0, 2)
    )
    grad_w_down = own_grads[2].reshape(local_experts, hidden_part, model_width)
    grad_out = mine(out_grad).astype(f32)
    grad_gain_two = jnp.sum(grad_normed_two * hat_two, axis=0)
    grad_middle = grad_out + rms_back(grad_normed_two * norm2_gain, hat_two, inv_two)
    grad_mid_low = lax.all_gather(grad_middle.astype(bf), "tensor", tiled=True)
    grad_out_weight = jnp.einsum("ti,td->id", mixed_low, grad_mid_low, preferred_element_type=f32)
    grad_mixed = (
        jnp.einsum("td,id->ti", grad_mid_low, out_weight, preferred_element_type=f32)
        .astype(bf)
        .reshape(tokens, local_heads, head_dim)
    )
    scores_again = (
        jnp.einsum("thd,sd->hts", query_low, key_low, preferred_element_type=f32) * score_scale
    )
    soft_again = jnp.where(visible[None], jnp.exp(scores_again - log_totals), 0.0)
    grad_soft = jnp.einsum("thd,sd->hts", grad_mixed, value_low, preferred_element_type=f32)
    grad_scores = (
        soft_again * (grad_soft - jnp.sum(soft_again * grad_soft, axis=-1, keepdims=True))
    ).astype(bf)
    grad_values = jnp.einsum(
        "hts,thd->sd", soft_again.astype(bf), grad_mixed, preferred_element_type=f32
    ).astype(bf)
    grad_query_rot = score_scale * jnp.einsum(
        "hts,sd->thd", grad_scores, key_low, preferred_element_type=f32
    )
    grad_key_rot = score_scale * jnp.einsum(
        "hts,thd->sd", grad_scores, query_low, preferred_element_type=f32
    )
    grad_query_norm = rotate_back(grad_query_rot, cosine_table[:, None, :], sine_table[:, None, :])
    grad_query_gain = jnp.sum(grad_query_norm * query_hat, axis=(0, 1))
    grad_query_low = (
        rms_back(grad_query_norm * query_gain, query_hat, query_inv)
        .reshape(tokens, local_heads * head_dim)
        .astype(bf)
    )
    grad_key_norm = rotate_back(grad_key_rot, cosine_table, sine_table)
    grad_key_gain = jnp.sum(grad_key_norm * key_hat, axis=0)
    grad_key_low = rms_back(grad_key_norm * key_gain, key_hat, key_inv).astype(bf)
    grad_query_weight = jnp.einsum("ti,tj->ij", normed, grad_query_low, preferred_element_type=f32)
    grad_key_weight = jnp.einsum("ti,tj->ij", normed, grad_key_low, preferred_element_type=f32)
    grad_value_weight = jnp.einsum("ti,tj->ij", normed, grad_values, preferred_element_type=f32)
    grad_normed_one = jnp.einsum(
        "tj,ij->ti", grad_query_low, query_weight, preferred_element_type=f32
    )
    grad_normed_one = grad_normed_one + jnp.einsum(
        "tj,ij->ti", grad_key_low, key_weight, preferred_element_type=f32
    )
    grad_normed_one = grad_normed_one + jnp.einsum(
        "tj,ij->ti", grad_values, value_weight, preferred_element_type=f32
    )
    grad_normed_one = lax.psum_scatter(grad_normed_one.astype(bf), "tensor", tiled=True).astype(f32)
    grad_gain_one = jnp.sum(grad_normed_one * hat_one_q, axis=0)
    grad_hidden = grad_middle + rms_back(grad_normed_one * norm1_gain, hat_one_q, inv_one_q)
    both = lax.all_gather(
        jnp.stack([hidden_out, grad_hidden.astype(bf)], axis=0), "tensor", axis=1, tiled=True
    )
    grad_out_sum = lax.psum(grad_out_weight.astype(bf), "dp").astype(f32)
    summed = (
        lax.psum(grad_query_weight.astype(bf), "dp").astype(f32),
        lax.psum(grad_key_weight.astype(bf), "dp").astype(f32),
        lax.psum(grad_value_weight.astype(bf), "dp").astype(f32),
    )
    gains = lax.psum(
        jnp.concatenate([grad_gain_one, grad_gain_two, grad_query_gain, grad_key_gain]),
        ("dp", "tensor"),
    )
    return (
        both[0],
        both[1],
        gains[:model_width],
        summed[0],
        summed[1],
        summed[2],
        gains[2 * model_width : 2 * model_width + head_dim],
        gains[2 * model_width + head_dim :],
        grad_out_sum,
        gains[model_width : 2 * model_width],
        grad_w_gate_up,
        grad_w_down,
    )


def solution(mesh):
    in_specs = (
        P("dp", None),
        P("dp", None),
        P(),
        P(None, "tensor"),
        P(None, "tensor"),
        P(None, "tensor"),
        P(),
        P(),
        P("tensor", None),
        P(),
        P("dp", None, None, "tensor"),
        P("dp", "tensor", None),
        P("dp", None),
        P("dp", None),
        P("dp", None),
    )
    out_specs = (
        P("dp", None),
        P("dp", None),
        P(),
        P(None, "tensor"),
        P(None, "tensor"),
        P(None, "tensor"),
        P(),
        P(),
        P("tensor", None),
        P(),
        P("dp", None, None, "tensor"),
        P("dp", "tensor", None),
    )
    return jax.shard_map(local, mesh=mesh, in_specs=in_specs, out_specs=out_specs, check_vma=False)
```

profile of v0, /device:TPU:0, one launch (start us, length us, event | category | flops | bytes accessed | tf_op | source)
XLA Modules:
  0.0 1135.6 jit_solution(16545600781011678941)
XLA Ops:
  10.0 2.6 fusion.15
  12.6 3.1 fusion.46
  15.7 2.4 fusion.93
  19.4 2.5 multiply_reduce_fusion.5
  26.9 2.6 fusion.7
  29.6 2.4 fusion.31
  34.9 3.7 convolution_convert_fusion.2
  44.3 2.2 copy.174
  46.7 2.6 pad_maximum_fusion.1
  49.3 23.3 %reduce-scatter.6.cloned.1.call-done = bf16[128,2048]{1,0:T(8,128)(2,1)} async-done(((bf16[512,2048]{1,0:T(8,128)(2,1)}), bf16[128,2048]{1,0:T(8,128)(2,1)}) %reduce-scatter.6.cloned.1.call-update) | async-done | bytes 524304 | tf_op jit(solution)/shard_map/reduce_scatter | solution.py:156
  76.4 46.4 %all-gather.7.cloned.1.call-done = bf16[1024,2080]{1,0:T(8,128)(2,1)} async-done(((bf16[128,2080]{1,0:T(8,128)(2,1)}), bf16[1024,2080]{1,0:T(8,128)(2,1)}) %all-gather.7.cloned.1.call-update) | async-done | bytes 4259856 | tf_op jit(solution)/shard_map/all_gather | solution.py:108
  127.2 3.0 copy.173
  130.2 113.1 %all-gather.15.cloned.1.call-done = bf16[12,384,2048]{2,1,0:T(8,128)(2,1)} async-done(((bf16[3,384,2048]{2,1,0:T(8,128)(2,1)}), bf16[12,384,2048]{2,1,0:T(8,128)(2,1)}) %all-gather.15.cloned.1.call-update) | async-done | bytes 18874384 | tf_op jit(solution)/shard_map/all_gather | solution.py:125
  243.3 12.0 %fusion.12 = f32[1024,4,384]{2,0,1:T(8,128)} fusion(bf16[4,3,384,2048]{3,2,1,0:T(8,128)(2,1)} %bitcast.231, bf16[1024,2080]{1,0:T(8,128)(2,1)} %all-gather.7.cloned.1.call-done), kind=kOutput, calls=%fused_computation.30 | convolution fusion | flops 6442450944 | bytes 16777216 | tf_op jit(solution)/shard_map/td,rud->tru/dot_general | solution.py:167
  255.3 63.2 %all-gather.9.cloned.1.call-done = bf16[1024,2048]{1,0:T(8,128)(2,1)} async-done(((bf16[128,2048]{1,0:T(8,128)(2,1)}), bf16[1024,2048]{1,0:T(8,128)(2,1)}) %all-gather.9.cloned.1.call-update) | async-done | bytes 4194320 | tf_op jit(solution)/shard_map/all_gather | solution.py:164
  318.4 11.8 %fusion.9 = f32[1024,4,384]{2,0,1:T(8,128)} fusion(bf16[4,3,384,2048]{3,2,1,0:T(8,128)(2,1)} %bitcast.232, bf16[1024,2048]{1,0:T(8,128)(2,1)} %all-gather.9.cloned.1.call-done), kind=kOutput, calls=%fused_computation.27 | convolution fusion | flops 6442450944 | bytes 16777216 | tf_op jit(solution)/shard_map/td,rud->tru/dot_general | solution.py:167
  330.3 15.8 %multiply_convert_fusion.2 = (bf16[1024,4,384]{2,0,1:T(8,128)(2,1)}, bf16[1024,4,384]{2,0,1:T(8,128)(2,1)S(1)}, bf16[1024,4,384]{2,0,1:T(8,128)(2,1)}) fusion(f32[1024,4,384]{2,0,1:T(8,128)} %fusion.9, f32[1024,384]{1,0:T(8,128)S(1)} %copy-done.21, f32[1024,4,384]{2,0,1:T(8,128)} %fusion.12, bf16[4,3,384,2048]{3,2,1,0:T(8,128)(2,1)} %bitcast.233, ...), kind=kOutput, calls=%fused_computation.24 | convolution fusion | flops 6470762496 | bytes 34078720 | tf_op jit(solution)/shard_map/td,rud->tru/dot_general | solution.py:167
  346.0 10.0 fusion.8
  356.1 10.3 fusion.3
  366.5 86.9 %reduce-scatter.10.cloned.1.call-done = bf16[128,2048]{1,0:T(8,128)(2,1)} async-done(((bf16[1024,2048]{1,0:T(8,128)(2,1)}), bf16[128,2048]{1,0:T(8,128)(2,1)}) %reduce-scatter.10.cloned.1.call-update) | async-done | bytes 524304 | tf_op jit(solution)/shard_map/reduce_scatter | solution.py:187
  453.3 2.3 fusion.53
  456.2 2.6 fusion.89
  462.3 18.8 %all-gather.11.cloned.1.call-done = bf16[512,2048]{1,0:T(8,128)(2,1)} async-done(((bf16[128,2048]{1,0:T(8,128)(2,1)}), bf16[512,2048]{1,0:T(8,128)(2,1)}) %all-gather.11.cloned.1.call-update) | async-done | bytes 2097168 | tf_op jit(solution)/shard_map/all_gather | solution.py:210
  481.2 5.3 fusion.35
  486.5 5.0 fusion
  491.6 2.7 fusion.2
  496.2 2.6 fusion.39
  501.5 3.2 fusion.64
  509.9 2.4 fusion.101
  516.1 11.0 bitcast_convert_fusion
  532.4 4.4 convolution_convert_fusion
  536.7 4.5 convolution_convert_fusion.1
  541.9 5.5 reduce-scatter.12.cloned.1.call-done
  548.8 90.9 %reduce-scatter.8.cloned.1.call-done = bf16[128,2048]{1,0:T(8,128)(2,1)} async-done(((bf16[1024,2048]{1,0:T(8,128)(2,1)}), bf16[128,2048]{1,0:T(8,128)(2,1)}) %reduce-scatter.8.cloned.1.call-update) | async-done | bytes 524304 | tf_op jit(solution)/shard_map/reduce_scatter | solution.py:177
  639.8 2.2 fusion.65
  643.4 9.8 convert_bitcast_fusion
  653.2 7.4 convert_bitcast_fusion.1
  660.6 7.4 convert_bitcast_fusion.2
  670.2 6.7 copy.190
  677.6 43.3 %psum.35 = f32[4352]{0:T(1024)S(1)} all-reduce(f32[4352]{0:T(1024)S(1)} %pad_maximum_fusion.8), channel_id=1, replica_groups=mesh['dp'=8,'tensor'=4] {'dp','tensor'}, use_global_device_ids=true, to_apply=%region_23.24 | all-reduce | flops 4352 | bytes 34816 | tf_op jit(solution)/shard_map/psum | solution.py:268
  722.1 221.7 %all-reduce.3.cloned.1.call-done = (bf16[2048,1024]{1,0:T(8,128)(2,1)}, bf16[2048,128]{1,0:T(8,128)(2,1)}, bf16[2048,128]{1,0:T(8,128)(2,1)}, bf16[1024,2048]{1,0:T(8,128)(2,1)}) async-done(((bf16[2048,1024]{1,0:T(8,128)(2,1)}, bf16[2048,128]{1,0:T(8,128)(2,1)}, bf16[2048,128]{1,0:T(8,128)(2,1)}, bf16[1024,2048]{1,0:T(8,128)(2,1)}), (bf16[2048,1024]{1,0:T(8,128)(2,1)}, bf16[2048,128]{1,0:T(8,128)(2,1)}, ...) | async-done | bytes 9437200 | tf_op jit(solution)/shard_map/psum | solution.py:264
  943.8 6.8 convert_element_type.187
  952.7 4.4 convert_element_type.193
  957.1 22.2 %all-gather.13.cloned.1.call-done = bf16[2,512,2048]{2,1,0:T(8,128)(2,1)} async-done(((bf16[2,128,2048]{2,1,0:T(8,128)(2,1)}), bf16[2,512,2048]{2,1,0:T(8,128)(2,1)}) %all-gather.13.cloned.1.call-update) | async-done | bytes 4194320 | tf_op jit(solution)/shard_map/all_gather | solution.py:259
  979.3 4.8 slice_bitcast_fusion.16
  984.1 135.6 %reduce-scatter.14.cloned.1.call-done = bf16[1152,2048]{1,0:T(8,128)(2,1)} async-done(((bf16[4608,2048]{1,0:T(8,128)(2,1)}), bf16[1152,2048]{1,0:T(8,128)(2,1)}) %reduce-scatter.14.cloned.1.call-update) | async-done | bytes 4718608 | tf_op jit(solution)/shard_map/reduce_scatter | solution.py:199
  1119.7 2.9 slice.113
  1122.6 3.1 copy.191
  (230 shorter events, 59.1 us)
Async XLA Ops:
  8.0 11.3 copy-start
  8.0 7.7 copy-start.35
  8.0 64.6 %reduce-scatter.6.cloned.1.call-start = ((), (), s32[]{:S(2)}) async-start(), calls=%async_computation.5 | async-start | bytes 2621440 | tf_op jit(solution)/shard_map/reduce_scatter | solution.py:156
  8.1 14.6 %copy-start.51 = (f32[64]{0:T(128)}, f32[64]{0:T(128)S(1)}, u32[]{:S(2)}) copy-start(f32[64]{0:T(128)S(1)} %multiply_exponential_fusion) | copy-start | bytes 772
  8.9 6.8 copy-start.3
  8.9 6.8 copy-start.57
  10.0 12.7 %copy-start.40 = (f32[512]{0:T(512)}, f32[512]{0:T(512)S(1)}, u32[]{:S(2)}) copy-start(f32[512]{0:T(512)S(1)} %subtract_convert_fusion.2) | copy-start | bytes 6148
  12.6 6.8 copy-start.49
  18.6 4.0 copy-start.47
  29.5 4.3 copy-start.2
  29.6 4.3 copy-start.43
  29.6 5.3 copy-start.56
  38.6 84.3 %all-gather.7.cloned.1.call-start = ((), (), s32[]{:S(2)}) async-start(), calls=%async_computation.6 | async-start | bytes 5013504 | tf_op jit(solution)/shard_map/all_gather | solution.py:108
  44.2 199.1 %all-gather.15.cloned.1.call-start = ((), (), s32[]{:S(2)}) async-start(), calls=%async_computation.14 | async-start | bytes 23592960 | tf_op jit(solution)/shard_map/all_gather | solution.py:125
  49.2 24.9 %copy-start.33 = (f32[2048]{0:T(1024)S(1)}, f32[2048]{0:T(1024)}, u32[]{:S(2)}) copy-start(f32[2048]{0:T(1024)} %param.24) | copy-start | bytes 24580
  49.3 269.2 %all-gather.9.cloned.1.call-start = ((), (), s32[]{:S(2)}) async-start(), calls=%async_computation.7 | async-start | bytes 4718592 | tf_op jit(solution)/shard_map/all_gather | solution.py:164
  74.1 50.1 %copy-start.44 = (f32[128]{0:T(128)}, f32[128]{0:T(128)S(1)}, u32[]{:S(2)}) copy-start(f32[128]{0:T(128)S(1)} %add_rsqrt_fusion.4) | copy-start | bytes 1540
  76.4 377.0 %reduce-scatter.10.cloned.1.call-start = ((), (), s32[]{:S(2)}) async-start(), calls=%async_computation.9 | async-start | bytes 4718592 | tf_op jit(solution)/shard_map/reduce_scatter | solution.py:187
  318.4 11.8 %copy-start.21 = (f32[1024,384]{1,0:T(8,128)S(1)}, f32[1024,384]{1,0:T(8,128)}, u32[]{:S(2)}) copy-start(f32[1024,384]{1,0:T(8,128)} %copy.173) | copy-start | bytes 4718596
  346.0 10.0 copy-start.63
  346.0 10.0 copy-start.65
  366.4 86.9 %copy-start.5 = (bf16[128,2048]{1,0:T(8,128)(2,1)S(1)}, bf16[128,2048]{1,0:T(8,128)(2,1)}, u32[]{:S(2)}) copy-start(bf16[128,2048]{1,0:T(8,128)(2,1)} %reduce-scatter.6.cloned.1.call-done) | copy-start | bytes 1572868
  366.4 114.8 %all-gather.11.cloned.1.call-start = ((), (), s32[]{:S(2)}) async-start(), calls=%async_computation.10 | async-start | bytes 2621440 | tf_op jit(solution)/shard_map/all_gather | solution.py:210
  458.9 88.5 %reduce-scatter.12.cloned.1.call-start = ((), (), s32[]{:S(2)}) async-start(), calls=%async_computation.11 | async-start | bytes 2621440 | tf_op jit(solution)/shard_map/reduce_scatter | solution.py:256
  481.2 5.3 copy-start.30
  481.2 5.4 copy-start.32
  481.2 10.4 slice-start
  486.5 5.1 slice-start.1
  501.4 4.1 copy-start.22
  516.0 123.7 %reduce-scatter.8.cloned.1.call-start = ((), (), s32[]{:S(2)}) async-start(), calls=%async_computation.8 | async-start | bytes 4718592 | tf_op jit(solution)/shard_map/reduce_scatter | solution.py:177
  527.1 416.6 %all-reduce.3.cloned.1.call-start = ((), (), s32[]{:S(2)}) async-start(), calls=%async_computation.15 | async-start | bytes 18874368 | tf_op jit(solution)/shard_map/psum | solution.py:264
  528.7 3.7 copy-start.60
  528.7 3.7 copy-start.62
  532.4 4.4 copy-start.24
  541.2 98.5 %copy-start.7 = (bf16[128,2048]{1,0:T(8,128)(2,1)S(1)}, bf16[128,2048]{1,0:T(8,128)(2,1)}, u32[]{:S(2)}) copy-start(bf16[128,2048]{1,0:T(8,128)(2,1)} %reduce-scatter.10.cloned.1.call-done) | copy-start | bytes 1572868
  541.2 98.5 %copy-start.34 = (f32[2048]{0:T(1024)S(1)}, f32[2048]{0:T(1024)}, u32[]{:S(2)}) copy-start(f32[2048]{0:T(1024)} %param.24) | copy-start | bytes 24580
  541.2 98.5 %copy-start.45 = (f32[128]{0:T(128)S(1)}, f32[128]{0:T(128)}, u32[]{:S(2)}) copy-start(f32[128]{0:T(128)} %copy-done.44) | copy-start | bytes 1540
  541.2 98.5 %copy-start.54 = (f32[128]{0:T(128)S(1)}, f32[128]{0:T(128)}, u32[]{:S(2)}) copy-start(f32[128]{0:T(128)} %copy-done.53) | copy-start | bytes 1540
  541.3 438.0 %all-gather.13.cloned.1.call-start = ((), (), s32[]{:S(2)}) async-start(), calls=%async_computation.12 | async-start | bytes 5242880 | tf_op jit(solution)/shard_map/all_gather | solution.py:259
  643.1 476.6 %reduce-scatter.14.cloned.1.call-start = ((), (), s32[]{:S(2)}) async-start(), calls=%async_computation.13 | async-start | bytes 23592960 | tf_op jit(solution)/shard_map/reduce_scatter | solution.py:199
  643.3 9.8 copy-start.59
  643.4 9.8 copy-start.66
  653.2 7.4 copy-start.64
  943.8 6.8 copy-start.27
  943.8 7.8 copy-start.26
  943.8 8.9 copy-start.8
  1119.7 6.0 slice-start.2
  1122.6 5.2 copy-start.1
  (34 other events, 65.3 us)
Sparse Core Ops, SparseCore 0:
  38.7 33.9 reduce-scatter.5
  459.0 22.1 all-gather.10
  516.1 31.1 reduce-scatter.11
  551.4 88.2 reduce-scatter.7
  645.2 298.5 all-reduce.2
  945.8 33.4 all-gather.12
  981.9 137.8 reduce-scatter.13
Sparse Core Ops, SparseCore 1:
  44.3 78.5 all-gather.6
  124.9 118.3 all-gather.14
  245.9 72.5 all-gather.8
  366.5 86.8 reduce-scatter.9
where the time goes:
time: 1140 us
  waiting for transfers between devices  828 us (73%)
  matrix products  146 us (13%)
  local copies, waits for them, and re-layouts  50.5 us (4%)
  other arithmetic  49.9 us (4%)
  blocking collectives  43.3 us (4%)
  between operations  17 us (1%)
    psum x1, waiting for transfers between devices, local(): lax.psum(grad_query_weight.astype(bf), 'dp').astype(f32)  222 us
    reduce_scatter x1, waiting for transfers between devices, local(): lax.psum_scatter(weight_grads.reshape(-1, model_width), 'tensor', tiled=T...  136 us
    all_gather x1, waiting for transfers between devices, local(): all_weights = lax.all_gather(own_weights, 'tensor')  113 us
    reduce_scatter x1, waiting for transfers between devices, local(): mixture = lax.psum_scatter(mixture_part, 'dp', tiled=True).astype(f32)  90.9 us
    reduce_scatter x1, waiting for transfers between devices, local(): lax.psum_scatter(grad_normed_part.astype(bf), 'dp', tiled=True).astype(f32)  86.9 us
    all_gather x1, waiting for transfers between devices, local(): inputs = lax.all_gather(normed_two, 'dp', tiled=True)  63.2 us
    all_gather x1, waiting for transfers between devices, local(): gathered = lax.all_gather(packed, 'dp', tiled=True)  46.4 us
    psum x1, blocking collectives, local(): lax.psum(jnp.concatenate([grad_gain_one, grad_gain_two, grad_query_gain,...  43.3 us
  transfers between devices with their start and end apart: 11, of which 11 were waited for; matrix products, arithmetic and copies ran while one was open for 10% of the time, Pallas kernels for 0%

commit v1 on v0

--- a/solution.py
+++ b/solution.py
@@ -6,6 +6,14 @@
 
 EPSILON = 1e-06
 ROPE_BASE = 1000000.0
+
+
+def panels_fill(vec, array_dim):
+    vec = jnp.moveaxis(vec, 0, array_dim)
+    met_up = vec.shape
+    return vec.reshape(
+        *met_up[:array_dim], met_up[array_dim] * met_up[array_dim + 1], *met_up[array_dim + 2 :]
+    )
 
 
 def rms_parts(values):
@@ -161,7 +169,21 @@
     middle = hidden_q + attention
     hat_two, inv_two = rms_parts(middle)
     normed_two = (hat_two * norm2_gain).astype(bf)
-    inputs = lax.all_gather(normed_two, "dp", tiled=True)
+    count_all = lax.axis_size("dp")
+    buffer = [(num, (num + 1) % count_all) for num in range(count_all)]
+    leaves = [(p, j0) for j0, p in buffer]
+    piece_out, oldest = ([], [])
+    for dev_i in [*range(count_all - 1)]:
+        if dev_i % 2 == 0:
+            piece_out.append(
+                lax.ppermute(piece_out[-1] if piece_out else normed_two, "dp", perm=buffer)
+            )
+        else:
+            oldest.append(lax.ppermute(oldest[-1] if oldest else normed_two, "dp", leaves))
+    carry = jnp.stack([*piece_out[::-1], normed_two, *oldest], axis=0)
+    high = lax.axis_index("dp") - len(piece_out)
+    carry = carry[(jnp.arange(count_all) - high) % count_all]
+    inputs = panels_fill(carry, 0)
 
     def project(left, which):
         return jnp.einsum("td,rud->tru", left, all_weights[:, which], preferred_element_type=f32)

time: 1140 us -> 1130 us (level)
  waiting for transfers between devices: 828 us -> 779 us
  local copies, waits for them, and re-layouts: 50.5 us -> 69 us
  starting transfers between devices: 0.85 us -> 19.1 us
    ppermute x0 -> x7, waiting for transfers between devices: none -> 89.3 us  [the longest x4 89.3 us: local(): lax.ppermute(piece_out[-1] if piece_out else normed_two, 'dp', perm=buffer)]
    all_gather x1 -> x0, waiting for transfers between devices: 63.2 us -> none  [local(): inputs = lax.all_gather(normed_two, 'dp', tiled=True)]
    all_gather x1, waiting for transfers between devices: 46.4 us -> 0.01 us  [local(): gathered = lax.all_gather(packed, 'dp', tiled=True)]
    all_gather x1, waiting for transfers between devices: 113 us -> 82.7 us  [local(): all_weights = lax.all_gather(own_weights, 'tensor')]
    ppermute x0 -> x7, starting transfers between devices: none -> 18.3 us  [the longest x3 14.1 us: local(): lax.ppermute(oldest[-1] if oldest else normed_two, 'dp', leaves)]
    unnamed x146 -> x157, local copies, waits for them, and re-layouts: 14.4 us -> 26.9 us
  transfers between devices with their start and end apart: 11 -> 17, of which waited for: 11 -> 13; matrix products, arithmetic and copies ran while one was open for 10% -> 11% of each run, Pallas kernels for 0% -> 0%
where the time goes in v1:
time: 1130 us; the launch traced here: 1120 us
  waiting for transfers between devices  779 us (69%)
  matrix products  147 us (13%)
  local copies, waits for them, and re-layouts  69 us (6%)
  other arithmetic  49.7 us (4%)
  blocking collectives  43.1 us (4%)
  starting transfers between devices  19.1 us (2%)
  between operations  17 us (2%)
    psum x1, waiting for transfers between devices, local(): lax.psum(grad_query_weight.astype(bf), 'dp').astype(f32)  222 us
    reduce_scatter x1, waiting for transfers between devices, local(): lax.psum_scatter(weight_grads.reshape(-1, model_width), 'tensor', tiled=T...  136 us
    reduce_scatter x1, waiting for transfers between devices, local(): mixture = lax.psum_scatter(mixture_part, 'dp', tiled=True).astype(f32)  91 us
    ppermute x4, waiting for transfers between devices, local(): lax.ppermute(piece_out[-1] if piece_out else normed_two, 'dp', perm=buffer)  89.3 us
    reduce_scatter x1, waiting for transfers between devices, local(): lax.psum_scatter(grad_normed_part.astype(bf), 'dp', tiled=True).astype(f32)  88.3 us
    all_gather x1, waiting for transfers between devices, local(): all_weights = lax.all_gather(own_weights, 'tensor')  82.7 us
    psum x1, blocking collectives, local(): lax.psum(jnp.concatenate([grad_gain_one, grad_gain_two, grad_query_gain,...  43.1 us
    dot_general x3, matrix products, project(): jnp.einsum('td,rud->tru', left, all_weights[:, which], preferred_element_...  39.9 us
  transfers between devices with their start and end apart: 17, of which 13 were waited for; matrix products, arithmetic and copies ran while one was open for 11% of the time, Pallas kernels for 0%

profile of v1, /device:TPU:0, one launch (start us, length us, event | category | flops | bytes accessed | tf_op | source)
XLA Modules:
  0.0 1123.1 jit_solution(1281838814658535848)
XLA Ops:
  10.0 2.6 fusion.15
  12.6 3.1 fusion.42
  19.3 2.5 multiply_reduce_fusion.5
  26.9 2.6 fusion.7
  34.8 3.7 convolution_convert_fusion.2
  46.6 2.6 pad_maximum_fusion.1
  49.3 23.3 %reduce-scatter.6.cloned.1.call-done = bf16[128,2048]{1,0:T(8,128)(2,1)} async-done(((bf16[512,2048]{1,0:T(8,128)(2,1)}), bf16[128,2048]{1,0:T(8,128)(2,1)}) %reduce-scatter.6.cloned.1.call-update) | async-done | bytes 524304 | tf_op jit(solution)/shard_map/reduce_scatter | solution.py:164
  77.1 21.4 %collective-permute-done = bf16[128,2048]{1,0:T(8,128)(2,1)S(1)} collective-permute-done((bf16[128,2048]{1,0:T(8,128)(2,1)S(1)}, bf16[128,2048]{1,0:T(8,128)(2,1)S(1)}, u32[]{:S(2)}, u32[]{:S(2)}) %collective-permute-start) | collective-permute-done | bytes 524320 | tf_op jit(solution)/shard_map/ppermute | solution.py:179
  98.6 4.5 collective-permute-start.4
  103.1 29.2 %collective-permute-done.1 = bf16[128,2048]{1,0:T(8,128)(2,1)S(1)} collective-permute-done((bf16[128,2048]{1,0:T(8,128)(2,1)S(1)}, bf16[128,2048]{1,0:T(8,128)(2,1)S(1)}, u32[]{:S(2)}, u32[]{:S(2)}) %collective-permute-start.1) | collective-permute-done | bytes 524320 | tf_op jit(solution)/shard_map/ppermute | solution.py:179
  134.8 4.9 collective-permute-start.5
  139.7 22.3 %collective-permute-done.2 = bf16[128,2048]{1,0:T(8,128)(2,1)} collective-permute-done((bf16[128,2048]{1,0:T(8,128)(2,1)S(1)}, bf16[128,2048]{1,0:T(8,128)(2,1)}, u32[]{:S(2)}, u32[]{:S(2)}) %collective-permute-start.2) | collective-permute-done | bytes 524320 | tf_op jit(solution)/shard_map/ppermute | solution.py:179
  162.6 4.7 collective-permute-start.6
  167.3 16.5 %collective-permute-done.3 = bf16[128,2048]{1,0:T(8,128)(2,1)} collective-permute-done((bf16[128,2048]{1,0:T(8,128)(2,1)}, bf16[128,2048]{1,0:T(8,128)(2,1)}, u32[]{:S(2)}, u32[]{:S(2)}) %collective-permute-start.3) | collective-permute-done | bytes 524320 | tf_op jit(solution)/shard_map/ppermute | solution.py:179
  197.1 5.2 gather_fusion
  206.5 3.0 copy.173
  209.5 82.7 %all-gather.12.cloned.1.call-done = bf16[12,384,2048]{2,1,0:T(8,128)(2,1)} async-done(((bf16[3,384,2048]{2,1,0:T(8,128)(2,1)}), bf16[12,384,2048]{2,1,0:T(8,128)(2,1)}) %all-gather.12.cloned.1.call-update) | async-done | bytes 18874384 | tf_op jit(solution)/shard_map/all_gather | solution.py:133
  292.3 11.9 %fusion.9 = f32[1024,4,384]{2,0,1:T(8,128)} fusion(bf16[1024,2048,1]{1,0,2:T(8,128)(2,1)} %bitcast.240, bf16[4,3,384,2048]{3,2,1,0:T(8,128)(2,1)} %bitcast.251), kind=kOutput, calls=%fused_computation.28 | convolution fusion | flops 6442450944 | bytes 16777216 | tf_op jit(solution)/shard_map/td,rud->tru/dot_general | solution.py:189
  304.1 11.9 %fusion.12 = f32[1024,4,384]{2,0,1:T(8,128)} fusion(bf16[4,3,384,2048]{3,2,1,0:T(8,128)(2,1)} %bitcast.252, bf16[1024,2080]{1,0:T(8,128)(2,1)} %all-gather.6.cloned.1.call-done), kind=kOutput, calls=%fused_computation.31 | convolution fusion | flops 6442450944 | bytes 16777216 | tf_op jit(solution)/shard_map/td,rud->tru/dot_general | solution.py:189
  316.0 16.2 %multiply_convert_fusion.2 = (bf16[1024,4,384]{2,0,1:T(8,128)(2,1)}, bf16[1024,4,384]{2,0,1:T(8,128)(2,1)}, bf16[1024,4,384]{2,0,1:T(8,128)(2,1)}) fusion(f32[1024,4,384]{2,0,1:T(8,128)} %fusion.9, f32[1024,384]{1,0:T(8,128)} %copy.173, f32[1024,4,384]{2,0,1:T(8,128)} %fusion.12, bf16[1024,2048,1]{1,0,2:T(8,128)(2,1)S(1)} %bitcast.242, ...), kind=kOutput, calls=%fused_computation.25 | convolution fusion | flops 6470762496 | bytes 34078720 | tf_op jit(solution)/shard_map/td,rud->tru/dot_general | solution.py:189
  332.2 9.9 fusion.8
  342.0 10.3 fusion.3
  352.4 88.3 %reduce-scatter.10.cloned.1.call-done = bf16[128,2048]{1,0:T(8,128)(2,1)} async-done(((bf16[1024,2048]{1,0:T(8,128)(2,1)}), bf16[128,2048]{1,0:T(8,128)(2,1)}) %reduce-scatter.10.cloned.1.call-update) | async-done | bytes 524304 | tf_op jit(solution)/shard_map/reduce_scatter | solution.py:209
  443.6 2.6 fusion.87
  449.7 18.9 %all-gather.8.cloned.1.call-done = bf16[512,2048]{1,0:T(8,128)(2,1)} async-done(((bf16[128,2048]{1,0:T(8,128)(2,1)}), bf16[512,2048]{1,0:T(8,128)(2,1)}) %all-gather.8.cloned.1.call-update) | async-done | bytes 2097168 | tf_op jit(solution)/shard_map/all_gather | solution.py:232
  468.6 5.3 fusion.31
  474.0 5.0 fusion
  479.1 2.7 fusion.2
  483.6 2.6 fusion.35
  488.9 3.2 fusion.60
  503.5 11.0 bitcast_convert_fusion
  519.8 4.4 convolution_convert_fusion
  524.2 4.5 convolution_convert_fusion.1
  529.3 5.4 reduce-scatter.12.cloned.1.call-done
  536.3 91.0 %reduce-scatter.8.cloned.1.call-done = bf16[128,2048]{1,0:T(8,128)(2,1)} async-done(((bf16[1024,2048]{1,0:T(8,128)(2,1)}), bf16[128,2048]{1,0:T(8,128)(2,1)}) %reduce-scatter.8.cloned.1.call-update) | async-done | bytes 524304 | tf_op jit(solution)/shard_map/reduce_scatter | solution.py:199
  630.8 10.0 convert_bitcast_fusion.1
  640.9 7.4 convert_bitcast_fusion.2
  648.3 7.3 convert_bitcast_fusion
  657.9 6.7 copy.190
  665.3 43.1 %psum.35 = f32[4352]{0:T(1024)S(1)} all-reduce(f32[4352]{0:T(1024)S(1)} %pad_maximum_fusion.8), channel_id=1, replica_groups=mesh['dp'=8,'tensor'=4] {'dp','tensor'}, use_global_device_ids=true, to_apply=%region_23.24 | all-reduce | flops 4352 | bytes 34816 | tf_op jit(solution)/shard_map/psum | solution.py:290
  709.5 221.8 %all-reduce.3.cloned.1.call-done = (bf16[2048,1024]{1,0:T(8,128)(2,1)}, bf16[2048,128]{1,0:T(8,128)(2,1)}, bf16[2048,128]{1,0:T(8,128)(2,1)}, bf16[1024,2048]{1,0:T(8,128)(2,1)}) async-done(((bf16[2048,1024]{1,0:T(8,128)(2,1)}, bf16[2048,128]{1,0:T(8,128)(2,1)}, bf16[2048,128]{1,0:T(8,128)(2,1)}, bf16[1024,2048]{1,0:T(8,128)(2,1)}), (bf16[2048,1024]{1,0:T(8,128)(2,1)}, bf16[2048,128]{1,0:T(8,128)(2,1)}, ...) | async-done | bytes 9437200 | tf_op jit(solution)/shard_map/psum | solution.py:286
  931.3 6.8 convert_element_type.187
  940.1 4.4 convert_element_type.193
  944.6 22.2 %all-gather.10.cloned.1.call-done = bf16[2,512,2048]{2,1,0:T(8,128)(2,1)} async-done(((bf16[2,128,2048]{2,1,0:T(8,128)(2,1)}), bf16[2,512,2048]{2,1,0:T(8,128)(2,1)}) %all-gather.10.cloned.1.call-update) | async-done | bytes 4194320 | tf_op jit(solution)/shard_map/all_gather | solution.py:281
  966.8 4.8 slice_bitcast_fusion.16
  971.6 135.6 %reduce-scatter.14.cloned.1.call-done = bf16[1152,2048]{1,0:T(8,128)(2,1)} async-done(((bf16[4608,2048]{1,0:T(8,128)(2,1)}), bf16[1152,2048]{1,0:T(8,128)(2,1)}) %reduce-scatter.14.cloned.1.call-update) | async-done | bytes 4718608 | tf_op jit(solution)/shard_map/reduce_scatter | solution.py:221
  1107.2 2.9 slice.115
  1110.1 3.1 copy.191
  (257 shorter events, 90.3 us)
Async XLA Ops:
  8.0 11.3 %copy-start = (bf16[2048,128]{1,0:T(8,128)(2,1)S(1)}, bf16[2048,128]{1,0:T(8,128)(2,1)}, u32[]{:S(2)}) copy-start(bf16[2048,128]{1,0:T(8,128)(2,1)} %param.19) | copy-start | bytes 1572868
  8.0 7.7 copy-start.37
  8.0 64.6 %reduce-scatter.6.cloned.1.call-start = ((), (), s32[]{:S(2)}) async-start(), calls=%async_computation.5 | async-start | bytes 2621440 | tf_op jit(solution)/shard_map/reduce_scatter | solution.py:164
  8.1 14.6 %copy-start.53 = (f32[64]{0:T(128)}, f32[64]{0:T(128)S(1)}, u32[]{:S(2)}) copy-start(f32[64]{0:T(128)S(1)} %multiply_exponential_fusion) | copy-start | bytes 772
  8.9 6.8 copy-start.3
  8.9 6.8 copy-start.59
  10.0 12.7 %copy-start.42 = (f32[512]{0:T(512)}, f32[512]{0:T(512)S(1)}, u32[]{:S(2)}) copy-start(f32[512]{0:T(512)S(1)} %subtract_convert_fusion.2) | copy-start | bytes 6148
  12.6 6.7 copy-start.51
  29.6 5.3 copy-start.58
  38.6 163.7 %all-gather.6.cloned.1.call-start = ((), (), s32[]{:S(2)}) async-start(), calls=%async_computation.6 | async-start | bytes 5013504 | tf_op jit(solution)/shard_map/all_gather | solution.py:116
  44.2 248.0 %all-gather.12.cloned.1.call-start = ((), (), s32[]{:S(2)}) async-start(), calls=%async_computation.13 | async-start | bytes 23592960 | tf_op jit(solution)/shard_map/all_gather | solution.py:133
  49.3 391.4 %reduce-scatter.10.cloned.1.call-start = ((), (), s32[]{:S(2)}) async-start(), calls=%async_computation.8 | async-start | bytes 4718592 | tf_op jit(solution)/shard_map/reduce_scatter | solution.py:209
  74.1 87.9 %copy-start.46 = (f32[128]{0:T(128)}, f32[128]{0:T(128)S(1)}, u32[]{:S(2)}) copy-start(f32[128]{0:T(128)S(1)} %add_rsqrt_fusion.4) | copy-start | bytes 1540
  75.5 22.9 %collective-permute-start = (bf16[128,2048]{1,0:T(8,128)(2,1)S(1)}, bf16[128,2048]{1,0:T(8,128)(2,1)S(1)}, u32[]{:S(2)}, u32[]{:S(2)}) collective-permute-start(bf16[128,2048]{1,0:T(8,128)(2,1)S(1)} %multiply_convert_fusion.3), channel_id=1, source_target_pairs={{0,4},{4,8},{8,12},{12,16},{16,20},{20,24},{24,28},{28,0},{1,5},{5... | collective-permute-start | bytes 1572872 | tf_op jit(solution)/shard_map/ppermute | solution.py:179
  98.4 36.4 %copy-start.29 = (bf16[128,2048]{1,0:T(8,128)(2,1)}, bf16[128,2048]{1,0:T(8,128)(2,1)S(1)}, u32[]{:S(2)}) copy-start(bf16[128,2048]{1,0:T(8,128)(2,1)S(1)} %collective-permute-done) | copy-start | bytes 1572868
  98.4 33.9 %collective-permute-start.1 = (bf16[128,2048]{1,0:T(8,128)(2,1)S(1)}, bf16[128,2048]{1,0:T(8,128)(2,1)S(1)}, u32[]{:S(2)}, u32[]{:S(2)}) collective-permute-start(bf16[128,2048]{1,0:T(8,128)(2,1)S(1)} %collective-permute-done), channel_id=1, source_target_pairs={{0,4},{4,8},{8,12},{12,16},{16,20},{20,24},{24,28},{28,0},{1,5},{5... | collective-permute-start | bytes 1572872 | tf_op jit(solution)/shard_map/ppermute | solution.py:179
  98.6 36.2 %collective-permute-start.4 = (bf16[128,2048]{1,0:T(8,128)(2,1)S(1)}, bf16[128,2048]{1,0:T(8,128)(2,1)}, u32[]{:S(2)}, u32[]{:S(2)}) collective-permute-start(bf16[128,2048]{1,0:T(8,128)(2,1)S(1)} %multiply_convert_fusion.3), channel_id=1, source_target_pairs={{4,0},{8,4},{12,8},{16,12},{20,16},{24,20},{28,24},{0,28},{5,1},{9... | collective-permute-start | bytes 1572872 | tf_op jit(solution)/shard_map/ppermute | solution.py:182
  132.3 7.4 copy-start.30
  132.3 29.6 %collective-permute-start.2 = (bf16[128,2048]{1,0:T(8,128)(2,1)S(1)}, bf16[128,2048]{1,0:T(8,128)(2,1)}, u32[]{:S(2)}, u32[]{:S(2)}) collective-permute-start(bf16[128,2048]{1,0:T(8,128)(2,1)S(1)} %collective-permute-done.1), channel_id=1, source_target_pairs={{0,4},{4,8},{8,12},{12,16},{16,20},{20,24},{24,28},{28,0},{1,5},{5... | collective-permute-start | bytes 1572872 | tf_op jit(solution)/shard_map/ppermute | solution.py:179
  134.8 27.8 %collective-permute-start.5 = (bf16[128,2048]{1,0:T(8,128)(2,1)}, bf16[128,2048]{1,0:T(8,128)(2,1)}, u32[]{:S(2)}, u32[]{:S(2)}) collective-permute-start(bf16[128,2048]{1,0:T(8,128)(2,1)} %collective-permute-done.4), channel_id=1, source_target_pairs={{4,0},{8,4},{12,8},{16,12},{20,16},{24,20},{28,24},{0,28},{5,1},{9... | collective-permute-start | bytes 1572872 | tf_op jit(solution)/shard_map/ppermute | solution.py:182
  162.0 21.8 %collective-permute-start.3 = (bf16[128,2048]{1,0:T(8,128)(2,1)}, bf16[128,2048]{1,0:T(8,128)(2,1)}, u32[]{:S(2)}, u32[]{:S(2)}) collective-permute-start(bf16[128,2048]{1,0:T(8,128)(2,1)} %collective-permute-done.2), channel_id=1, source_target_pairs={{0,4},{4,8},{8,12},{12,16},{16,20},{20,24},{24,28},{28,0},{1,5},{5... | collective-permute-start | bytes 1572872 | tf_op jit(solution)/shard_map/ppermute | solution.py:179
  162.6 33.6 %collective-permute-start.6 = (bf16[128,2048]{1,0:T(8,128)(2,1)}, bf16[128,2048]{1,0:T(8,128)(2,1)S(1)}, u32[]{:S(2)}, u32[]{:S(2)}) collective-permute-start(bf16[128,2048]{1,0:T(8,128)(2,1)} %collective-permute-done.5), channel_id=1, source_target_pairs={{4,0},{8,4},{12,8},{16,12},{20,16},{24,20},{28,24},{0,28},{5,1},{9... | collective-permute-start | bytes 1572872 | tf_op jit(solution)/shard_map/ppermute | solution.py:182
  304.1 11.9 %copy-start.9 = (bf16[8,128,2048]{2,1,0:T(8,128)(2,1)S(1)}, bf16[8,128,2048]{2,1,0:T(8,128)(2,1)}, u32[]{:S(2)}) copy-start(bf16[8,128,2048]{2,1,0:T(8,128)(2,1)} %gather_fusion) | copy-start | bytes 12582916
  332.2 9.9 copy-start.65
  352.3 88.3 %copy-start.5 = (bf16[128,2048]{1,0:T(8,128)(2,1)S(1)}, bf16[128,2048]{1,0:T(8,128)(2,1)}, u32[]{:S(2)}) copy-start(bf16[128,2048]{1,0:T(8,128)(2,1)} %reduce-scatter.6.cloned.1.call-done) | copy-start | bytes 1572868
  352.4 116.2 %all-gather.8.cloned.1.call-start = ((), (), s32[]{:S(2)}) async-start(), calls=%async_computation.9 | async-start | bytes 2621440 | tf_op jit(solution)/shard_map/all_gather | solution.py:232
  446.3 88.5 %reduce-scatter.12.cloned.1.call-start = ((), (), s32[]{:S(2)}) async-start(), calls=%async_computation.10 | async-start | bytes 2621440 | tf_op jit(solution)/shard_map/reduce_scatter | solution.py:278
  468.6 5.3 copy-start.33
  468.6 5.4 copy-start.35
  468.6 10.4 slice-start
  503.5 123.8 %reduce-scatter.8.cloned.1.call-start = ((), (), s32[]{:S(2)}) async-start(), calls=%async_computation.7 | async-start | bytes 4718592 | tf_op jit(solution)/shard_map/reduce_scatter | solution.py:199
  514.6 416.7 %all-reduce.3.cloned.1.call-start = ((), (), s32[]{:S(2)}) async-start(), calls=%async_computation.14 | async-start | bytes 18874368 | tf_op jit(solution)/shard_map/psum | solution.py:286
  528.7 98.6 %copy-start.7 = (bf16[128,2048]{1,0:T(8,128)(2,1)S(1)}, bf16[128,2048]{1,0:T(8,128)(2,1)}, u32[]{:S(2)}) copy-start(bf16[128,2048]{1,0:T(8,128)(2,1)} %reduce-scatter.10.cloned.1.call-done) | copy-start | bytes 1572868
  528.7 98.6 %copy-start.36 = (f32[2048]{0:T(1024)S(1)}, f32[2048]{0:T(1024)}, u32[]{:S(2)}) copy-start(f32[2048]{0:T(1024)} %param.24) | copy-start | bytes 24580
  528.7 98.6 %copy-start.47 = (f32[128]{0:T(128)S(1)}, f32[128]{0:T(128)}, u32[]{:S(2)}) copy-start(f32[128]{0:T(128)} %copy-done.46) | copy-start | bytes 1540
  528.7 98.6 %copy-start.56 = (f32[128]{0:T(128)S(1)}, f32[128]{0:T(128)}, u32[]{:S(2)}) copy-start(f32[128]{0:T(128)} %copy-done.55) | copy-start | bytes 1540
  528.7 438.0 %all-gather.10.cloned.1.call-start = ((), (), s32[]{:S(2)}) async-start(), calls=%async_computation.11 | async-start | bytes 5242880 | tf_op jit(solution)/shard_map/all_gather | solution.py:281
  630.6 476.6 %reduce-scatter.14.cloned.1.call-start = ((), (), s32[]{:S(2)}) async-start(), calls=%async_computation.12 | async-start | bytes 23592960 | tf_op jit(solution)/shard_map/reduce_scatter | solution.py:221
  630.8 10.0 copy-start.10
  630.8 10.0 copy-start.64
  630.8 17.5 %slice-start.4 = ((s8[4456448]{0:T(1024)(128)(4,1)}), s8[4194304]{0:T(1024)(128)(4,1)S(1)}, s32[]{:S(2)}) async-start(s8[4456448]{0:T(1024)(128)(4,1)} %bitcast.246), calls=%async_computation.19 | async-start | bytes 8388608
  640.9 7.5 slice-start.5
  640.9 7.5 copy-start.66
  931.2 6.8 copy-start.28
  931.2 7.8 copy-start.27
  931.3 8.9 copy-start.8
  1107.2 6.0 slice-start.2
  1110.1 5.2 copy-start.1
  (42 other events, 98.7 us)
Sparse Core Ops, SparseCore 0:
  38.7 33.9 reduce-scatter.5
  446.4 22.1 all-gather.7
  503.6 31.1 reduce-scatter.11
  538.8 88.3 reduce-scatter.7
  632.7 298.5 all-reduce.2
  933.2 33.4 all-gather.9
  969.3 137.8 reduce-scatter.13
Sparse Core Ops, SparseCore 1:
  44.3 117.9 all-gather.5
  164.3 127.9 all-gather.11
  352.5 88.2 reduce-scatter.9
